TPU v7x, 256 devices: a whole 4x4x8 slice. The times are simulated.
256 devices in a mesh: seq: 32 (over z, x), exp: 8 (over y, core).
Axes of the slice: x: 4, y: 4, z: 8, core: 2. Of those that a mesh axis runs over, the one named last changes fastest.
Arguments:
- tokens: bfloat16 [32768, 2560], P(('seq', 'exp')), may hold values from -6 to 6
- routes: int32 [32768, 1], P(('seq', 'exp')), may hold values from 0 to 15; in each aligned block of 128 rows (0 to 127, 128 to 255, ...) at most 16 rows name the same one
- gate_inner_weight: bfloat16 [2560, 2, 3072], P(None, None, 'exp'), may hold values from -0.125 to 0.125
- state_map_weight: bfloat16 [2560, 256], replicated, may hold values from -0.125 to 0.125
- step_size_weight: bfloat16 [2560, 48], P(None, 'exp'), may hold values from -0.125 to 0.125
- adapter_down_weight: bfloat16 [2560, 128], P(None, 'exp'), may hold values from -0.125 to 0.125
- adapter_up_weight: bfloat16 [128, 2, 3072], P(None, None, 'exp'), may hold values from -1.5 to 1.5
- inner_conv_taps: float32 [4, 3072], P(None, 'exp'), may hold values from -3 to 3
- state_map_taps: float32 [4, 256], replicated, may hold values from -3 to 3
- inner_conv_bias: float32 [3072], P('exp'), may hold values from -3 to 3
- state_map_conv_bias: float32 [256], replicated, may hold values from -3 to 3
- step_size_bias: float32 [48], P('exp'), may hold values from -6 to -3
- head_decay_rate: float32 [48], P('exp'), may hold values from 4.656613e-06 to 8
- direct_head_scale: float32 [48], P('exp'), may hold values from 0.5 to 2
- gated_norm_scale: float32 [3072], P('exp'), may hold values from 0.5 to 1.5
Outputs:
- mixed: bfloat16 [32768, 3072], P('seq', 'exp')
Inputs may be any that keep to these rules, and one draw needn't show every extreme that they name: `routes`: among the rows of one device no expert is named more than 16 times.
All inputs are finite; a program needn't handle non-finite values.
Results may differ from a plain program's by a relative error of at most 0.0034.
Values may be sent and summed in bfloat16 or wider, within the bound.
A program may use at most 64 MiB of HBM per device.

v0:
```python
import jax
import jax.numpy as jnp
from jax import lax
from jax.sharding import Mesh
from jax.sharding import PartitionSpec as P

STATE = 128
HEADDIM = 64
ADAPTER_EXPERTS = 16
EXPERT_RANK = 8
GROUP = 256
INNER_WIDTH = 3072
SEQ = ("seq_0", "seq_1")
SEQ_EXP = ("seq_0", "seq_1", "exp")
HIGH = lax.Precision.HIGHEST


def laid_out(parts, dim):
    lengths = list(parts.shape[1:])
    lengths[dim] *= parts.shape[0]
    return jnp.moveaxis(parts, 0, dim).reshape(lengths)


def copy_for_each(value, axis):
    size = lax.axis_size(axis)
    return lax.all_to_all(
        jnp.broadcast_to(value[None], (size, *value.shape)), axis, 0, 0, tiled=True
    )


def gathered_copies(value, axis, dim):
    return laid_out(copy_for_each(value, axis), dim)


def passed_along(block, axis, distance):
    devices = range(lax.axis_size(axis))
    route = [(i - distance, i) for i in devices if i - distance in devices]
    return lax.ppermute(block, axis, route)


def filled_with(value, identity):
    return jax.tree.map(
        lambda a, e: jnp.broadcast_to(jnp.asarray(e, a.dtype), a.shape), value, identity
    )


def entering_2(value, axes, combine, identity):
    before = start = filled_with(value, identity)
    running = value
    for axis in reversed(axes):
        size, index = (lax.axis_size(axis), lax.axis_index(axis))
        pieces = jax.tree.map(lambda part: lax.all_gather(part, axis), running)
        inside, running = (start, start)
        for k in range(size):
            passed = k < index
            running = combine(running, jax.tree.map(lambda part: part[k], pieces))
            inside = jax.tree.map(lambda new, old: jnp.where(passed, new, old), running, inside)
        before = combine(inside, before)
    return before


def taken_together(value, axis):
    return copy_for_each(value, axis).sum(axis=0)


def block_step(state, items):
    inner, bmap, cmap, step, decay = items
    cumul = jnp.cumsum(decay, axis=0)
    length = decay.shape[0]
    rows = lax.broadcasted_iota(jnp.int32, (length, length), 0)
    cols = lax.broadcasted_iota(jnp.int32, (length, length), 1)
    causal = (rows >= cols)[:, :, None]
    differ = jnp.where(causal, cumul[:, None, :] - cumul[None, :, :], 0.0)
    segment = jnp.where(causal, jnp.exp(differ), 0.0)
    gram = jnp.dot(cmap, bmap.T, precision=HIGH)
    weights = gram[:, :, None] * segment * step[None, :, :]
    output = jnp.einsum("ijh,jhp->ihp", weights, inner, precision=HIGH)
    output = output + jnp.exp(cumul)[:, :, None] * jnp.einsum(
        "in,hnp->ihp", cmap, state, precision=HIGH
    )
    final = cumul[-1]
    carried = jnp.exp(final[None, :] - cumul) * step
    update = jnp.einsum("jn,jhp->hnp", bmap, carried[:, :, None] * inner, precision=HIGH)
    return (jnp.exp(final)[:, None, None] * state + update, output)


def run_blocks(inner, bmap, cmap, step, decay, state, block):
    total = inner.shape[0]
    count_blocks = total // block
    items = (
        inner.reshape(count_blocks, block, inner.shape[1], inner.shape[2]),
        bmap.reshape(count_blocks, block, bmap.shape[1]),
        cmap.reshape(count_blocks, block, cmap.shape[1]),
        step.reshape(count_blocks, block, step.shape[1]),
        decay.reshape(count_blocks, block, decay.shape[1]),
    )
    final, output = lax.scan(block_step, state, items)
    return (final, output.reshape(total, inner.shape[1], inner.shape[2]))


def causal_conv(extended, weights, bias):
    length = extended.shape[0] - weights.shape[0] + 1
    output = bias[None, :] + jnp.zeros((length, weights.shape[1]), jnp.float32)
    for shift_idx in range(weights.shape[0]):
        output = output + weights[shift_idx][None, :] * extended[shift_idx : shift_idx + length]
    return jax.nn.silu(output)


def pick_ranks(partial_columns, route, experts, width):
    column_expert = lax.broadcasted_iota(jnp.int32, (experts * width,), 0) // width
    masked = jnp.where(route[:, None] == column_expert[None, :], partial_columns, 0.0)
    return jnp.sum(masked.reshape(partial_columns.shape[0], experts, width), axis=1)


def lift_ranks(ranks, route, experts):
    width = ranks.shape[1]
    column_expert = lax.broadcasted_iota(jnp.int32, (experts * width,), 0) // width
    repeated_tiles = jnp.tile(ranks, (1, experts))
    return jnp.where(
        route[:, None] == column_expert[None, :], repeated_tiles, jnp.zeros_like(repeated_tiles)
    )


def body(
    tokens,
    routes,
    gate_inner_weight,
    state_map_weight,
    step_size_weight,
    adapter_down_weight,
    adapter_up_weight,
    inner_conv_taps,
    state_map_taps,
    inner_conv_bias,
    state_map_conv_bias,
    step_size_bias,
    head_decay_rate,
    direct_head_scale,
    gated_norm_scale,
):
    whole, route_all = (
        lax.all_gather(tokens, "exp", axis=0, tiled=True),
        lax.all_gather(routes, "exp", axis=0, tiled=True),
    )
    route_flat = route_all[:, 0]
    all_down_maps = gathered_copies(adapter_down_weight, "exp", 1)
    partial_columns = jnp.dot(whole, all_down_maps, preferred_element_type=jnp.float32)
    ranks = pick_ranks(partial_columns, route_flat, ADAPTER_EXPERTS, EXPERT_RANK).astype(
        jnp.bfloat16
    )
    length = whole.shape[0]
    features = whole.shape[1]
    split_widths = gate_inner_weight.shape[2]
    raised_values = lift_ranks(ranks, route_flat, ADAPTER_EXPERTS)
    gate_inner_values = jnp.dot(
        whole,
        gate_inner_weight.reshape(features, 2 * split_widths),
        preferred_element_type=jnp.float32,
    )
    gate_inner_values = gate_inner_values + jnp.dot(
        raised_values,
        adapter_up_weight.reshape(ADAPTER_EXPERTS * EXPERT_RANK, 2 * split_widths),
        preferred_element_type=jnp.float32,
    )
    gate = gate_inner_values[:, :split_widths]
    inner = gate_inner_values[:, split_widths:]
    bc_raw = jnp.dot(whole, state_map_weight, preferred_element_type=jnp.float32)
    dt_raw = jnp.dot(whole, step_size_weight, preferred_element_type=jnp.float32)
    margin = inner_conv_taps.shape[0] - 1
    inner_rim, bc_rim = passed_along((inner[length - margin :], bc_raw[length - margin :]), SEQ, 1)
    xconv = causal_conv(
        jnp.concatenate([inner_rim, inner], axis=0), inner_conv_taps, inner_conv_bias
    )
    bconv = causal_conv(
        jnp.concatenate([bc_rim, bc_raw], axis=0), state_map_taps, state_map_conv_bias
    )
    bmap = bconv[:, :STATE]
    cmap = bconv[:, STATE:]
    step = jax.nn.softplus(dt_raw + step_size_bias[None, :])
    decay = -head_decay_rate[None, :] * step
    heads = head_decay_rate.shape[0]
    heads_in = xconv.reshape(length, heads, HEADDIM)
    empty_state = jnp.zeros((heads, STATE, HEADDIM), jnp.float32)
    final, output = run_blocks(heads_in, bmap, cmap, step, decay, empty_state, GROUP)
    factor = jnp.exp(jnp.sum(decay, axis=0))

    def combine(earlier, later):
        return (earlier[0] * later[0], later[0][:, None, None] * earlier[1] + later[1])

    total_decay, entering = entering_2(
        (factor, final), SEQ, combine, (jnp.ones((heads,), jnp.float32), empty_state)
    )
    cumul = jnp.cumsum(decay, axis=0)
    output = output + jnp.exp(cumul)[:, :, None] * jnp.einsum(
        "in,hnp->ihp", cmap, entering, precision=HIGH
    )
    output = output + direct_head_scale[None, :, None] * heads_in
    gated = output.reshape(length, split_widths) * jax.nn.silu(gate)
    squares = taken_together(jnp.sum(gated * gated, axis=1), "exp")
    scale = lax.rsqrt(squares / INNER_WIDTH + 1e-05)
    return (gated * scale[:, None] * gated_norm_scale[None, :]).astype(jnp.bfloat16)


def solution(mesh):
    split = Mesh(mesh.devices.reshape(8, 4, mesh.shape["exp"]), ("seq_0", "seq_1", "exp"))
    in_specs = (
        P(SEQ_EXP, None),
        P(SEQ_EXP, None),
        P(None, None, "exp"),
        P(),
        P(None, "exp"),
        P(None, "exp"),
        P(None, None, "exp"),
        P(None, "exp"),
        P(),
        P("exp"),
        P(),
        P("exp"),
        P("exp"),
        P("exp"),
        P("exp"),
    )
    out_specs = P(SEQ, "exp")
    return jax.shard_map(body, mesh=split, in_specs=in_specs, out_specs=out_specs, check_vma=False)
```

profile of v0, /device:TPU:1, one launch (start us, length us, event | category | flops | bytes accessed | tf_op | source)
XLA Modules:
  0.0 258.2 jit_solution(6099084624724914850)
XLA Ops:
  6.5 0.7 all-gather.6.cloned.1.call-update
  7.3 1.8 broadcast_in_dim.72
  9.0 6.6 %all-to-all-start = ((bf16[8,2560,16]{1,2,0:T(8,128)(2,1)}), bf16[8,2560,16]{1,2,0:T(8,128)(2,1)S(1)}, u32[]{:S(2)}, u32[]{:S(2)}) async-start(bf16[8,2560,16]{1,2,0:T(8,128)(2,1)} %broadcast_in_dim.72), calls=%async_computation | async-start | bytes 1310720 | tf_op jit(solution)/shard_map/all_to_all | solution.py:26
  15.7 4.8 %copy.123 = bf16[320,8,2,384]{3,1,2,0:T(8,128)(2,1)} copy(bf16[320,8,2,384]{3,2,1,0:T(2,128)(2,1)} %bitcast.267) | data formatting | bytes 7864320
  21.8 11.0 %all_gather.25 = s32[1024,1]{0,1:T(1,128)S(1)} all-gather(s32[128,1]{0,1:T(1,128)S(1)} %copy-done.18), channel_id=1, replica_groups=mesh['seq_0'=8,'seq_1'=4,'exp'=8] {'exp'}, dimensions={0}, use_global_device_ids=true | all-gather | bytes 4608 | tf_op jit(solution)/shard_map/all_gather | solution.py:143
  32.9 19.5 %all-gather.6.cloned.1.call-done = bf16[1024,2560]{1,0:T(8,128)(2,1)} async-done(((bf16[128,2560]{1,0:T(8,128)(2,1)}), bf16[1024,2560]{1,0:T(8,128)(2,1)}) %all-gather.6.cloned.1.call-update) | async-done | bytes 5242896 | tf_op jit(solution)/shard_map/all_gather | solution.py:142
  52.4 9.5 %fusion.98 = f32[1024,768]{1,0:T(8,128)} fusion(bf16[1024,2560]{1,0:T(8,128)(2,1)} %all-gather.6.cloned.1.call-done, bf16[2560,768]{1,0:T(8,128)(2,1)} %bitcast.268), kind=kOutput, calls=%fused_computation.167 | convolution fusion | flops 4026531840 | bytes 12320768 | tf_op jit(solution)/shard_map/dot_general | solution.py:155
  61.9 4.4 %fusion.54 = bf16[1024,8]{0,1:T(8,128)(2,1)S(1)} fusion(bf16[1024,2560]{1,0:T(8,128)(2,1)} %all-gather.6.cloned.1.call-done, bf16[2560,128]{0,1:T(8,128)(2,1)S(1)} %bitcast.271, s32[1024]{0:T(1024)S(1)} %bitcast.281, s32[128]{0:T(128)S(1)} %and_select_fusion), kind=kOutput, calls=%fused_computation.70 | convolution fusion | flops 671473664 | bytes 5919232 | tf_op jit(solution)/shard_map/dot_general | solution.py:147
  66.4 0.7 convolution_add_fusion
  67.1 1.6 copy-done.3
  68.8 3.2 %collective-permute-start = (f32[3,384]{1,0:T(4,128)S(1)}, f32[3,384]{1,0:T(4,128)S(1)}, u32[]{:S(2)}, u32[]{:S(2)}) collective-permute-start(f32[3,384]{1,0:T(4,128)S(1)} %slice.215), channel_id=1, source_target_pairs={{0,8},{8,16},{16,24},{24,32},{32,40},{40,48},{48,56},{56,64},{64,7... | collective-permute-start | bytes 13832 | tf_op jit(solution)/shard_map/ppermute | solution.py:38
  72.0 1.5 fusion.99
  73.6 3.1 %collective-permute-start.1 = (f32[3,256]{1,0:T(4,128)S(1)}, f32[3,256]{1,0:T(4,128)S(1)}, u32[]{:S(2)}, u32[]{:S(2)}) collective-permute-start(f32[3,256]{1,0:T(4,128)S(1)} %slice.221), channel_id=1, source_target_pairs={{0,8},{8,16},{16,24},{24,32},{32,40},{40,48},{48,56},{56,64},{64,7... | collective-permute-start | bytes 9224 | tf_op jit(solution)/shard_map/ppermute | solution.py:38
  76.7 1.6 fusion.95
  78.4 8.6 %all-reduce = f32[24]{0:T(128)S(1)} all-reduce(f32[24]{0:T(128)S(1)} %exponential_dynamic-update-slice_fusion), channel_id=2, replica_groups=mesh['seq_0'=8,'seq_1'=4,'exp'=8] {'seq_1'}, use_global_device_ids=true, to_apply=%add | all-reduce | flops 24 | bytes 192
  87.1 0.7 copy-done.16
  87.8 0.7 divide_multiply_fusion.1
  88.4 1.0 copy-done.5
  89.4 1.1 fusion.96
  90.5 0.7 slice-done
  91.2 2.2 divide_multiply_fusion
  93.4 1.9 copy.104
  95.3 1.9 reshape_reshape.3
  97.2 81.9 %while.13 = (s32[]{:T(128)}, f32[6,128,64]{1,2,0:T(8,128)S(1)}, f32[4,256,6,64]{1,0,3,2:T(4,128)}, f32[4,256,6]{1,2,0:T(8,128)S(1)}, f32[4,256,6]{1,2,0:T(8,128)...) while((s32[]{:T(128)}, f32[6,128,64]{1,2,0:T(8,128)S(1)}, ...), condition=%wide.region_4.5_spmd.clone, body=%wide.region_1.4_spmd.clone.sunk | while | flops 707316736 | bytes 6607687 | solution.py:97
  97.2 1.8 reduce-window.26
  99.7 1.4 fusion.133
  101.1 1.4 fusion.132
  102.5 1.8 constant_dynamic-slice_fusion.2
  104.3 2.0 fusion.134
  106.7 9.5 %dynamic_update_slice.6 = f32[4,256,6,64]{1,0,3,2:T(4,128)} dynamic-update-slice(f32[4,256,6,64]{1,0,3,2:T(4,128)} %get-tuple-element.250, f32[1,256,6,64]{1,0,3,2:T(1,128)S(1)} %copy.158, s32[]{:T(128)} %get-tuple-element.248, s32[]{:T(128)} %constant.71.clone.1..sunk, s32[]{:T(128)} %constant.71.clone.1..sunk, s32[]{:T(128)} %constant.71.clone.1..sunk) | dynamic-update-slice | bytes 786436 | tf_op jit(solution)/shard_map/while/body/jit(dynamic_update_index_in_dim)/dynamic_update_slice | solution.py:97
  116.2 1.4 fusion.131
  117.7 1.8 reduce-window.26
  120.2 1.4 fusion.133
  121.6 1.3 fusion.132
  122.9 1.8 constant_dynamic-slice_fusion.2
  124.8 2.0 fusion.134
  127.2 9.5 %dynamic_update_slice.6 = f32[4,256,6,64]{1,0,3,2:T(4,128)} dynamic-update-slice(f32[4,256,6,64]{1,0,3,2:T(4,128)} %get-tuple-element.250, f32[1,256,6,64]{1,0,3,2:T(1,128)S(1)} %copy.158, s32[]{:T(128)} %get-tuple-element.248, s32[]{:T(128)} %constant.71.clone.1..sunk, s32[]{:T(128)} %constant.71.clone.1..sunk, s32[]{:T(128)} %constant.71.clone.1..sunk) | dynamic-update-slice | bytes 786436 | tf_op jit(solution)/shard_map/while/body/jit(dynamic_update_index_in_dim)/dynamic_update_slice | solution.py:97
  136.7 1.4 fusion.131
  138.1 1.8 reduce-window.26
  140.7 1.4 fusion.133
  142.1 1.4 fusion.132
  143.4 1.8 constant_dynamic-slice_fusion.2
  145.3 2.0 fusion.134
  147.7 9.5 %dynamic_update_slice.6 = f32[4,256,6,64]{1,0,3,2:T(4,128)} dynamic-update-slice(f32[4,256,6,64]{1,0,3,2:T(4,128)} %get-tuple-element.250, f32[1,256,6,64]{1,0,3,2:T(1,128)S(1)} %copy.158, s32[]{:T(128)} %get-tuple-element.248, s32[]{:T(128)} %constant.71.clone.1..sunk, s32[]{:T(128)} %constant.71.clone.1..sunk, s32[]{:T(128)} %constant.71.clone.1..sunk) | dynamic-update-slice | bytes 786436 | tf_op jit(solution)/shard_map/while/body/jit(dynamic_update_index_in_dim)/dynamic_update_slice | solution.py:97
  157.2 1.4 fusion.131
  158.6 1.8 reduce-window.26
  161.1 1.4 fusion.133
  162.5 1.3 fusion.132
  163.9 1.8 constant_dynamic-slice_fusion.2
  165.7 2.0 fusion.134
  168.1 9.5 %dynamic_update_slice.6 = f32[4,256,6,64]{1,0,3,2:T(4,128)} dynamic-update-slice(f32[4,256,6,64]{1,0,3,2:T(4,128)} %get-tuple-element.250, f32[1,256,6,64]{1,0,3,2:T(1,128)S(1)} %copy.158, s32[]{:T(128)} %get-tuple-element.248, s32[]{:T(128)} %constant.71.clone.1..sunk, s32[]{:T(128)} %constant.71.clone.1..sunk, s32[]{:T(128)} %constant.71.clone.1..sunk) | dynamic-update-slice | bytes 786436 | tf_op jit(solution)/shard_map/while/body/jit(dynamic_update_index_in_dim)/dynamic_update_slice | solution.py:97
  177.6 1.4 fusion.131
  179.0 11.5 %all-gather.1 = f32[24,128,64]{1,2,0:T(8,128)S(1)} all-gather(f32[6,128,64]{1,2,0:T(8,128)S(1)} %get-tuple-element.49), channel_id=3, replica_groups=mesh['seq_0'=8,'seq_1'=4,'exp'=8] {'seq_1'}, dimensions={0}, use_global_device_ids=true | all-gather | bytes 983040 | tf_op jit(solution)/shard_map/all_gather | solution.py:52
  190.6 0.8 bitcast_add_fusion
  191.5 1.7 reduce-window.16
  193.6 12.4 %all-gather.2 = f32[8,1,6]{2,1,0:T(1,128)S(1)} all-gather(f32[1,1,6]{2,1,0:T(1,128)S(1)} %get-tuple-element.177), channel_id=1, replica_groups=mesh['seq_0'=8,'seq_1'=4,'exp'=8] {'seq_0'}, dimensions={0}, use_global_device_ids=true | all-gather | bytes 216 | tf_op jit(solution)/shard_map/all_gather | solution.py:52
  206.0 2.9 %reshape.225 = f32[1024,6,64]{0,2,1:T(8,128)} reshape(f32[4,256,6,64]{1,0,3,2:T(4,128)} %get-tuple-element.48) | data formatting | bytes 3145728 | tf_op jit(solution)/shard_map/reshape | solution.py:98
  208.9 19.9 %all-gather.8.cloned.1.call-done = f32[8,6,128,64]{2,3,1,0:T(8,128)} async-done(((f32[1,6,128,64]{2,3,1,0:T(8,128)}), f32[8,6,128,64]{2,3,1,0:T(8,128)}) %all-gather.8.cloned.1.call-update) | async-done | bytes 1572880 | tf_op jit(solution)/shard_map/all_gather | solution.py:52
  228.8 2.0 fusion.71
  230.8 1.4 fusion.93
  232.8 1.6 copy.110
  234.5 2.5 multiply_reduce_fusion
  236.9 13.3 %all_to_all.11 = f32[8,1,1024]{2,1,0:T(1,128)S(1)} all-to-all(f32[8,1,1024]{2,1,0:T(1,128)S(1)} %broadcast_in_dim.77), channel_id=1, replica_groups=mesh['seq_0'=8,'seq_1'=4,'exp'=8] {'exp'}, dimensions={0} | all-to-all | bytes 65536 | tf_op jit(solution)/shard_map/all_to_all | solution.py:26
  250.3 1.1 multiply_convert_fusion
  (131 shorter events, 6.6 us)
Async XLA Ops:
  6.5 65.5 %copy-start = (bf16[2560,256]{1,0:T(8,128)(2,1)S(1)}, bf16[2560,256]{1,0:T(8,128)(2,1)}, u32[]{:S(2)}) copy-start(bf16[2560,256]{1,0:T(8,128)(2,1)} %param.20) | copy-start | bytes 3932164
  6.5 45.9 %all-gather.6.cloned.1.call-start = ((), (), s32[]{:S(2)}) async-start(), calls=%async_computation.2 | async-start | bytes 5898240 | tf_op jit(solution)/shard_map/all_gather | solution.py:142
  9.0 52.9 %all-to-all-start = ((bf16[8,2560,16]{1,2,0:T(8,128)(2,1)}), bf16[8,2560,16]{1,2,0:T(8,128)(2,1)S(1)}, u32[]{:S(2)}, u32[]{:S(2)}) async-start(bf16[8,2560,16]{1,2,0:T(8,128)(2,1)} %broadcast_in_dim.72), calls=%async_computation | async-start | bytes 1310720 | tf_op jit(solution)/shard_map/all_to_all | solution.py:26
  15.7 213.2 %all-gather.8.cloned.1.call-start = ((), (), s32[]{:S(2)}) async-start(), calls=%async_computation.3 | async-start | bytes 1769472 | tf_op jit(solution)/shard_map/all_gather | solution.py:52
  15.7 4.9 %copy-start.9 = (bf16[128,2,384]{2,1,0:T(2,128)(2,1)S(1)}, bf16[128,2,384]{2,1,0:T(2,128)(2,1)}, u32[]{:S(2)}) copy-start(bf16[128,2,384]{2,1,0:T(2,128)(2,1)} %param.23) | copy-start | bytes 589828
  15.7 4.9 %copy-start.19 = (f32[6]{0:T(128)S(1)}, f32[6]{0:T(128)}, u32[]{:S(2)}) copy-start(f32[6]{0:T(128)} %param.29) | copy-start | bytes 76
  15.7 5.0 %copy-start.20 = (u32[256]{0:T(256)S(1)}, u32[256]{0:T(256)}, u32[]{:S(2)}) copy-start(u32[256]{0:T(256)} %constant.97) | copy-start | bytes 3076
  15.7 6.1 %copy-start.18 = (s32[128,1]{0,1:T(1,128)S(1)}, s32[128,1]{0,1:T(1,128)}, u32[]{:S(2)}) copy-start(s32[128,1]{0,1:T(1,128)} %param.18) | copy-start | bytes 1540
  15.7 17.1 %copy-start.11 = (f32[4,384]{1,0:T(4,128)S(1)}, f32[4,384]{1,0:T(4,128)}, u32[]{:S(2)}) copy-start(f32[4,384]{1,0:T(4,128)} %param.24) | copy-start | bytes 18436
  15.7 17.1 %copy-start.12 = (f32[4,256]{1,0:T(4,128)S(1)}, f32[4,256]{1,0:T(4,128)}, u32[]{:S(2)}) copy-start(f32[4,256]{1,0:T(4,128)} %param.25) | copy-start | bytes 12292
  61.9 4.4 %copy-start.8 = (f32[1024,768]{1,0:T(8,128)S(1)}, f32[1024,768]{1,0:T(8,128)}, u32[]{:S(2)}) copy-start(f32[1024,768]{1,0:T(8,128)} %fusion.98) | copy-start | bytes 9437188
  66.4 5.6 %copy-start.4 = (bf16[1024,2560]{1,0:T(8,128)(2,1)S(1)}, bf16[1024,2560]{1,0:T(8,128)(2,1)}, u32[]{:S(2)}) copy-start(bf16[1024,2560]{1,0:T(8,128)(2,1)} %all-gather.6.cloned.1.call-done) | copy-start | bytes 15728644
  67.1 1.7 copy-start.3
  68.8 7.9 %copy-start.10 = (bf16[2560,6]{0,1:T(8,128)(2,1)S(1)}, bf16[2560,6]{0,1:T(8,128)(2,1)}, u32[]{:S(2)}) copy-start(bf16[2560,6]{0,1:T(8,128)(2,1)} %param.21) | copy-start | bytes 92164
  68.8 7.9 %copy-start.14 = (f32[6]{0:T(128)S(1)}, f32[6]{0:T(128)}, u32[]{:S(2)}) copy-start(f32[6]{0:T(128)} %param.28) | copy-start | bytes 76
  68.8 21.7 %collective-permute-start = (f32[3,384]{1,0:T(4,128)S(1)}, f32[3,384]{1,0:T(4,128)S(1)}, u32[]{:S(2)}, u32[]{:S(2)}) collective-permute-start(f32[3,384]{1,0:T(4,128)S(1)} %slice.215), channel_id=1, source_target_pairs={{0,8},{8,16},{16,24},{24,32},{32,40},{40,48},{48,56},{56,64},{64,7... | collective-permute-start | bytes 13832 | tf_op jit(solution)/shard_map/ppermute | solution.py:38
  73.6 13.5 %collective-permute-start.1 = (f32[3,256]{1,0:T(4,128)S(1)}, f32[3,256]{1,0:T(4,128)S(1)}, u32[]{:S(2)}, u32[]{:S(2)}) collective-permute-start(f32[3,256]{1,0:T(4,128)S(1)} %slice.221), channel_id=1, source_target_pairs={{0,8},{8,16},{16,24},{24,32},{32,40},{40,48},{48,56},{56,64},{64,7... | collective-permute-start | bytes 9224 | tf_op jit(solution)/shard_map/ppermute | solution.py:38
  87.1 0.7 copy-start.16
  88.4 1.0 copy-start.5
  89.4 1.8 slice-start
  89.4 1.8 copy-start.13
  95.3 1.9 copy-start.1
  208.9 21.9 %copy-start.6 = (f32[1024,256]{1,0:T(8,128)S(1)}, f32[1024,256]{1,0:T(8,128)}, u32[]{:S(2)}) copy-start(f32[1024,256]{1,0:T(8,128)} %copy-done.5) | copy-start | bytes 3145732
  228.8 3.4 %copy-start.7 = (f32[1024,6,64]{0,2,1:T(8,128)S(1)}, f32[1024,6,64]{0,2,1:T(8,128)}, u32[]{:S(2)}) copy-start(f32[1024,6,64]{0,2,1:T(8,128)} %reshape.225) | copy-start | bytes 4718596
  230.8 1.5 copy-start.2
  230.8 1.5 copy-start.17
  234.5 15.8 %copy-start.15 = (f32[384]{0:T(512)S(1)}, f32[384]{0:T(512)}, u32[]{:S(2)}) copy-start(f32[384]{0:T(512)} %param.31) | copy-start | bytes 4612
Sparse Core Ops, SparseCore 0:
  9.2 43.2 all-gather.5
  191.5 37.2 all-gather.7
where the time goes:
time: 260 us; the launch traced here: 258 us
  local copies, waits for them, and re-layouts  69.9 us (27%)
  blocking collectives  56.9 us (22%)
  matrix products  43.5 us (17%)
  waiting for transfers between devices  40.2 us (15%)
  other arithmetic  20.2 us (8%)
  between operations  14.4 us (6%)
  starting transfers between devices  13 us (5%)
    dynamic_update_slice x8, local copies, waits for them, and re-layouts, run_blocks(): final, output = lax.scan(block_step, state, items)  39.7 us
    all_gather x2, blocking collectives, entering_2(): pieces = jax.tree.map(lambda part: lax.all_gather(part, axis), running)  23.9 us
    all_gather x1, waiting for transfers between devices, entering_2(): pieces = jax.tree.map(lambda part: lax.all_gather(part, axis), running)  19.9 us
    all_gather x1, waiting for transfers between devices, body(): lax.all_gather(tokens, 'exp', axis=0, tiled=True)  19.5 us
    all_to_all x1, blocking collectives, copy_for_each(): lax.all_to_all(jnp.broadcast_to(value[None], (size, *value.shape)), axis,...  13.3 us
    all_gather x1, blocking collectives, body(): lax.all_gather(routes, 'exp', axis=0, tiled=True)  11 us
    dot_general x1, matrix products, body(): jnp.dot(whole, gate_inner_weight.reshape(features, 2 * split_widths), pre...  9.51 us
    another operation x10, other arithmetic  9.32 us
  transfers between devices with their start and end apart: 5, of which 2 were waited for; matrix products, arithmetic and copies ran while one was open for 10% of the time, Pallas kernels for 0%

commit v1 on v0

--- a/solution.py
+++ b/solution.py
@@ -13,6 +13,27 @@
 SEQ = ("seq_0", "seq_1")
 SEQ_EXP = ("seq_0", "seq_1", "exp")
 HIGH = lax.Precision.HIGHEST
+
+
+def collect(x, axis, dim):
+    size, place, rows = (lax.axis_size(axis), lax.axis_index(axis), x.shape[dim])
+    right = [(i, (i + 1) % size) for i in range(size)]
+    backward = [(i, (i - 1) % size) for i in range(size)]
+    out = jnp.zeros((*x.shape[:dim], size * rows, *x.shape[dim + 1 :]), x.dtype)
+    out = lax.dynamic_update_slice_in_dim(out, x, place * rows, axis=dim)
+    from_left = from_right = x
+    half = size // 2
+    for step in range(1, half + 1):
+        from_left = lax.ppermute(from_left, axis, right)
+        out = lax.dynamic_update_slice_in_dim(
+            out, from_left, (place - step) % size * rows, axis=dim
+        )
+        if step < size - half:
+            from_right = lax.ppermute(from_right, axis, backward)
+            out = lax.dynamic_update_slice_in_dim(
+                out, from_right, (place + step) % size * rows, axis=dim
+            )
+    return out
 
 
 def laid_out(parts, dim):
@@ -139,7 +160,7 @@
     gated_norm_scale,
 ):
     whole, route_all = (
-        lax.all_gather(tokens, "exp", axis=0, tiled=True),
+        collect(tokens, "exp", 0),
         lax.all_gather(routes, "exp", axis=0, tiled=True),
     )
     route_flat = route_all[:, 0]

time: 260 us -> 301 us (1.16)
  local copies, waits for them, and re-layouts: 69.9 us -> 84.9 us
  other arithmetic: 20.2 us -> 29.3 us
  starting transfers between devices: 13 us -> 20.9 us
  blocking collectives: 56.9 us -> 62.7 us
    all_gather x1 -> x0, waiting for transfers between devices: 19.5 us -> none  [body(): lax.all_gather(tokens, 'exp', axis=0, tiled=True)]
    ppermute x0 -> x7, waiting for transfers between devices: none -> 14.7 us  [the longest x4 14.6 us: collect(): from_left = lax.ppermute(from_left, axis, right)]
    ppermute x0 -> x7, starting transfers between devices: none -> 9.84 us  [the longest x4 7.53 us: collect(): from_left = lax.ppermute(from_left, axis, right)]
    dynamic_update_slice x0 -> x8, local copies, waits for them, and re-layouts: none -> 8.2 us  [the longest x4 4.65 us: collect(): lax.dynamic_update_slice_in_dim(out, from_left, (place - step) % size * r...]
    all_gather x1, waiting for transfers between devices: 19.9 us -> 25.6 us  [entering_2(): pieces = jax.tree.map(lambda part: lax.all_gather(part, axis), running)]
    all_gather x1, blocking collectives: 11 us -> 15.9 us  [body(): lax.all_gather(routes, 'exp', axis=0, tiled=True)]
    dot_general x1, matrix products: 9.51 us -> 6.16 us  [body(): jnp.dot(whole, gate_inner_weight.reshape(features, 2 * split_widths), pre...]
    dot_general x1, matrix products: 1.59 us -> 4.67 us  [body(): jnp.dot(whole, step_size_weight, preferred_element_type=jnp.float32)]
  transfers between devices with their start and end apart: 5 -> 11, of which waited for: 2 -> 5; matrix products, arithmetic and copies ran while one was open for 10% -> 11% of each run, Pallas kernels for 0% -> 0%
where the time goes in v1:
time: 301 us; the launch traced here: 299 us
  local copies, waits for them, and re-layouts  84.9 us (28%)
  blocking collectives  62.7 us (21%)
  matrix products  45.7 us (15%)
  waiting for transfers between devices  40.3 us (13%)
  other arithmetic  29.3 us (10%)
  starting transfers between devices  20.9 us (7%)
  between operations  14.7 us (5%)
    dynamic_update_slice x8, local copies, waits for them, and re-layouts, run_blocks(): final, output = lax.scan(block_step, state, items)  39.7 us
    all_gather x1, waiting for transfers between devices, entering_2(): pieces = jax.tree.map(lambda part: lax.all_gather(part, axis), running)  25.6 us
    all_gather x2, blocking collectives, entering_2(): pieces = jax.tree.map(lambda part: lax.all_gather(part, axis), running)  24.5 us
    all_gather x1, blocking collectives, body(): lax.all_gather(routes, 'exp', axis=0, tiled=True)  15.9 us
    ppermute x4, waiting for transfers between devices, collect(): from_left = lax.ppermute(from_left, axis, right)  14.6 us
    all_to_all x1, blocking collectives, copy_for_each(): lax.all_to_all(jnp.broadcast_to(value[None], (size, *value.shape)), axis,...  13.3 us
    another operation x10, other arithmetic  11.7 us
    unnamed x1, blocking collectives  8.96 us
  transfers between devices with their start and end apart: 11, of which 5 were waited for; matrix products, arithmetic and copies ran while one was open for 11% of the time, Pallas kernels for 0%

profile of v1, /device:TPU:1, one launch (start us, length us, event | category | flops | bytes accessed | tf_op | source)
XLA Modules:
  0.0 298.9 jit_solution(10646274630234138494)
XLA Ops:
  6.5 2.7 collective-permute-start
  9.8 1.8 broadcast_in_dim.76
  11.5 6.4 %all-to-all-start = ((bf16[8,2560,16]{1,2,0:T(8,128)(2,1)}), bf16[8,2560,16]{1,2,0:T(8,128)(2,1)S(1)}, u32[]{:S(2)}, u32[]{:S(2)}) async-start(bf16[8,2560,16]{1,2,0:T(8,128)(2,1)} %broadcast_in_dim.76), calls=%async_computation | async-start | bytes 1310720 | tf_op jit(solution)/shard_map/all_to_all | solution.py:47
  18.1 15.9 %all_gather.21 = s32[1024,1]{0,1:T(1,128)S(1)} all-gather(s32[128,1]{0,1:T(1,128)S(1)} %copy-done.29), channel_id=1, replica_groups=mesh['seq_0'=8,'seq_1'=4,'exp'=8] {'exp'}, dimensions={0}, use_global_device_ids=true | all-gather | bytes 4608 | tf_op jit(solution)/shard_map/all_gather | solution.py:164
  34.0 4.7 %copy.123 = bf16[320,8,2,384]{3,1,2,0:T(8,128)(2,1)} copy(bf16[320,8,2,384]{3,2,1,0:T(2,128)(2,1)} %bitcast.267) | data formatting | bytes 7864320
  40.2 2.6 broadcast_in_dim.75
  44.3 2.0 constant_dynamic-update-slice_fusion.6
  47.1 4.5 %collective-permute-done.2 = bf16[128,2560]{1,0:T(8,128)(2,1)S(1)} collective-permute-done((bf16[128,2560]{1,0:T(8,128)(2,1)}, bf16[128,2560]{1,0:T(8,128)(2,1)S(1)}, u32[]{:S(2)}, u32[]{:S(2)}) %collective-permute-start.2) | collective-permute-done | bytes 655392 | tf_op jit(solution)/shard_map/ppermute | solution.py:27
  51.6 2.4 collective-permute-start.4
  57.1 4.4 %collective-permute-done.4 = bf16[128,2560]{1,0:T(8,128)(2,1)S(1)} collective-permute-done((bf16[128,2560]{1,0:T(8,128)(2,1)S(1)}, bf16[128,2560]{1,0:T(8,128)(2,1)S(1)}, u32[]{:S(2)}, u32[]{:S(2)}) %collective-permute-start.4) | collective-permute-done | bytes 655392 | tf_op jit(solution)/shard_map/ppermute | solution.py:27
  61.5 2.5 collective-permute-start.6
  65.8 5.7 %collective-permute-done.6 = bf16[128,2560]{1,0:T(8,128)(2,1)S(1)} collective-permute-done((bf16[128,2560]{1,0:T(8,128)(2,1)S(1)}, bf16[128,2560]{1,0:T(8,128)(2,1)S(1)}, u32[]{:S(2)}, u32[]{:S(2)}) %collective-permute-start.6) | collective-permute-done | bytes 655392 | tf_op jit(solution)/shard_map/ppermute | solution.py:27
  72.4 4.4 %fusion.54 = bf16[1024,8]{0,1:T(8,128)(2,1)S(1)} fusion(bf16[1024,2560]{1,0:T(8,128)(2,1)} %constant_dynamic-update-slice_fusion, bf16[2560,128]{0,1:T(8,128)(2,1)S(1)} %bitcast.271, s32[1024]{0:T(1024)S(1)} %bitcast.280, s32[128]{0:T(128)S(1)} %and_select_fusion), kind=kOutput, calls=%fused_computation.70 | convolution fusion | flops 671473664 | bytes 5919232 | tf_op jit(solution)/shard_map/dot_general | solution.py:168
  77.5 6.2 %convolution_add_fusion = f32[1024,768]{1,0:T(8,128)S(1)} fusion(f32[1024,768]{1,0:T(8,128)S(1)} %fusion.65, bf16[1024,2560]{1,0:T(8,128)(2,1)} %constant_dynamic-update-slice_fusion, bf16[2560,768]{1,0:T(8,128)(2,1)S(1)} %bitcast.268), kind=kOutput, calls=%fused_computation.50 | convolution fusion | flops 4027318272 | bytes 15466496 | tf_op jit(solution)/shard_map/dot_general | solution.py:176
  83.8 1.5 collective-permute-start.7
  85.3 4.0 %fusion.99 = f32[1024,256]{1,0:T(8,128)S(1)} fusion(bf16[1024,2560]{1,0:T(8,128)(2,1)} %constant_dynamic-update-slice_fusion, bf16[2560,256]{1,0:T(8,128)(2,1)S(1)} %copy-done), kind=kOutput, calls=%fused_computation.176 | convolution fusion | flops 1342177280 | bytes 7602176 | tf_op jit(solution)/shard_map/dot_general | solution.py:188
  89.3 3.1 %collective-permute-start.8 = (f32[3,256]{1,0:T(4,128)S(1)}, f32[3,256]{1,0:T(4,128)S(1)}, u32[]{:S(2)}, u32[]{:S(2)}) collective-permute-start(f32[3,256]{1,0:T(4,128)S(1)} %slice.221), channel_id=1, source_target_pairs={{0,8},{8,16},{16,24},{24,32},{32,40},{40,48},{48,56},{56,64},{64,7... | collective-permute-start | bytes 9224 | tf_op jit(solution)/shard_map/ppermute | solution.py:59
  92.5 4.7 %fusion.96 = (f32[6]{0:T(128)S(1)}, f32[1024,6]{0,1:T(8,128)S(1)}, f32[1024,6]{0,1:T(8,128)S(1)}, f32[1024,6]{0,1:T(8,128)}) fusion(f32[6]{0:T(128)S(1)} %neg.22, f32[6]{0:T(128)S(1)} %copy-done.23, bf16[1024,2560]{1,0:T(8,128)(2,1)} %constant_dynamic-update-slice_fusion, bf16[2560,6]{0,1:T(8,128)(2,1)S(1)} %copy-done.13), kind=kOutput, calls=%fused_computation.173 | convolution fusion | flops 31512570 | bytes 5347400 | tf_op jit(solution)/shard_map/dot_general | solution.py:189
  97.3 9.0 %all-reduce = f32[24]{0:T(128)S(1)} all-reduce(f32[24]{0:T(128)S(1)} %exponential_dynamic-update-slice_fusion), channel_id=2, replica_groups=mesh['seq_0'=8,'seq_1'=4,'exp'=8] {'seq_1'}, use_global_device_ids=true, to_apply=%add | all-reduce | flops 24 | bytes 192
  111.1 2.1 divide_multiply_fusion
  113.2 1.9 copy.104
  115.1 1.9 reshape_reshape.3
  117.0 91.1 %while.13 = (s32[]{:T(128)}, f32[6,128,64]{1,2,0:T(8,128)S(1)}, f32[4,256,6,64]{1,0,3,2:T(4,128)}, f32[4,256,6]{1,2,0:T(8,128)S(1)}, f32[4,256,6]{1,2,0:T(8,128)...) while((s32[]{:T(128)}, f32[6,128,64]{1,2,0:T(8,128)S(1)}, ...), condition=%wide.region_4.5_spmd.clone, body=%wide.region_1.4_spmd.clone.sunk | while | flops 707316736 | bytes 6656011 | solution.py:118
  117.0 1.8 constant_dynamic-slice_fusion.2
  118.8 1.8 reduce-window.26
  123.6 1.4 fusion.131
  125.0 1.3 fusion.132
  126.4 1.4 fusion.133
  127.8 2.0 fusion.134
  130.2 9.5 %dynamic_update_slice.46 = f32[4,256,6,64]{1,0,3,2:T(4,128)} dynamic-update-slice(f32[4,256,6,64]{1,0,3,2:T(4,128)} %get-tuple-element.250, f32[1,256,6,64]{1,0,3,2:T(1,128)S(1)} %copy.158, s32[]{:T(128)S(6)} %copy.171, s32[]{:T(128)} %constant.113.clone.1..sunk, s32[]{:T(128)} %constant.113.clone.1..sunk, s32[]{:T(128)} %constant.113.clone.1..sunk) | dynamic-update-slice | bytes 786436 | tf_op jit(solution)/shard_map/while/body/jit(dynamic_update_index_in_dim)/dynamic_update_slice | solution.py:118
  139.7 1.8 constant_dynamic-slice_fusion.2
  141.6 1.8 reduce-window.26
  146.4 1.4 fusion.131
  147.8 1.4 fusion.132
  149.2 1.4 fusion.133
  150.6 2.0 fusion.134
  153.0 9.5 %dynamic_update_slice.46 = f32[4,256,6,64]{1,0,3,2:T(4,128)} dynamic-update-slice(f32[4,256,6,64]{1,0,3,2:T(4,128)} %get-tuple-element.250, f32[1,256,6,64]{1,0,3,2:T(1,128)S(1)} %copy.158, s32[]{:T(128)S(6)} %copy.171, s32[]{:T(128)} %constant.113.clone.1..sunk, s32[]{:T(128)} %constant.113.clone.1..sunk, s32[]{:T(128)} %constant.113.clone.1..sunk) | dynamic-update-slice | bytes 786436 | tf_op jit(solution)/shard_map/while/body/jit(dynamic_update_index_in_dim)/dynamic_update_slice | solution.py:118
  162.5 1.8 constant_dynamic-slice_fusion.2
  164.4 1.8 reduce-window.26
  169.2 1.4 fusion.131
  170.6 1.3 fusion.132
  172.0 1.4 fusion.133
  173.4 2.0 fusion.134
  175.8 9.5 %dynamic_update_slice.46 = f32[4,256,6,64]{1,0,3,2:T(4,128)} dynamic-update-slice(f32[4,256,6,64]{1,0,3,2:T(4,128)} %get-tuple-element.250, f32[1,256,6,64]{1,0,3,2:T(1,128)S(1)} %copy.158, s32[]{:T(128)S(6)} %copy.171, s32[]{:T(128)} %constant.113.clone.1..sunk, s32[]{:T(128)} %constant.113.clone.1..sunk, s32[]{:T(128)} %constant.113.clone.1..sunk) | dynamic-update-slice | bytes 786436 | tf_op jit(solution)/shard_map/while/body/jit(dynamic_update_index_in_dim)/dynamic_update_slice | solution.py:118
  185.3 1.8 constant_dynamic-slice_fusion.2
  187.1 1.8 reduce-window.26
  192.0 1.4 fusion.131
  193.4 1.4 fusion.132
  194.8 1.4 fusion.133
  196.2 2.0 fusion.134
  198.5 9.5 %dynamic_update_slice.46 = f32[4,256,6,64]{1,0,3,2:T(4,128)} dynamic-update-slice(f32[4,256,6,64]{1,0,3,2:T(4,128)} %get-tuple-element.250, f32[1,256,6,64]{1,0,3,2:T(1,128)S(1)} %copy.158, s32[]{:T(128)S(6)} %copy.171, s32[]{:T(128)} %constant.113.clone.1..sunk, s32[]{:T(128)} %constant.113.clone.1..sunk, s32[]{:T(128)} %constant.113.clone.1..sunk) | dynamic-update-slice | bytes 786436 | tf_op jit(solution)/shard_map/while/body/jit(dynamic_update_index_in_dim)/dynamic_update_slice | solution.py:118
  208.1 10.6 %all-gather.1 = f32[24,128,64]{1,2,0:T(8,128)S(1)} all-gather(f32[6,128,64]{1,2,0:T(8,128)S(1)} %get-tuple-element.49), channel_id=3, replica_groups=mesh['seq_0'=8,'seq_1'=4,'exp'=8] {'seq_1'}, dimensions={0}, use_global_device_ids=true | all-gather | bytes 983040 | tf_op jit(solution)/shard_map/all_gather | solution.py:73
  219.5 1.5 bitcast_add_fusion
  221.1 1.7 reduce-window.16
  223.3 14.0 %all-gather.2 = f32[8,1,6]{2,1,0:T(1,128)S(1)} all-gather(f32[1,1,6]{2,1,0:T(1,128)S(1)} %copy-done.24), channel_id=1, replica_groups=mesh['seq_0'=8,'seq_1'=4,'exp'=8] {'seq_0'}, dimensions={0}, use_global_device_ids=true | all-gather | bytes 216 | tf_op jit(solution)/shard_map/all_gather | solution.py:73
  237.3 2.9 reshape.225
  240.2 25.6 %all-gather.5.cloned.1.call-done = f32[8,6,128,64]{2,3,1,0:T(8,128)} async-done(((f32[1,6,128,64]{2,3,1,0:T(8,128)}), f32[8,6,128,64]{2,3,1,0:T(8,128)}) %all-gather.5.cloned.1.call-update) | async-done | bytes 1572880 | tf_op jit(solution)/shard_map/all_gather | solution.py:73
  265.8 2.2 fusion.72
  268.0 1.4 fusion.94
  269.5 1.7 multiply_add_fusion
  271.2 1.9 copy.110
  273.1 3.1 %multiply_reduce_fusion = (f32[1024]{0:T(1024)S(1)}, f32[1024,384]{1,0:T(8,128)}) fusion(f32[1024,384]{1,0:T(8,128)S(1)} %copy.110, f32[1024,768]{1,0:T(8,128)} %copy-done.4), kind=kLoop, calls=%fused_computation.62 | loop fusion | flops 2751488 | bytes 4722688 | tf_op jit(solution)/shard_map/reduce_sum | solution.py:220
  276.2 13.3 %all_to_all.11 = f32[8,1,1024]{2,1,0:T(1,128)S(1)} all-to-all(f32[8,1,1024]{2,1,0:T(1,128)S(1)} %broadcast_in_dim.81), channel_id=1, replica_groups=mesh['seq_0'=8,'seq_1'=4,'exp'=8] {'exp'}, dimensions={0} | all-to-all | bytes 65536 | tf_op jit(solution)/shard_map/all_to_all | solution.py:47
  289.5 2.5 multiply_convert_fusion
  (191 shorter events, 30.2 us)
Async XLA Ops:
  6.5 78.8 %copy-start = (bf16[2560,256]{1,0:T(8,128)(2,1)S(1)}, bf16[2560,256]{1,0:T(8,128)(2,1)}, u32[]{:S(2)}) copy-start(bf16[2560,256]{1,0:T(8,128)(2,1)} %param.20) | copy-start | bytes 3932164
  6.5 11.5 %copy-start.10 = (bf16[128,2,384]{2,1,0:T(2,128)(2,1)S(1)}, bf16[128,2,384]{2,1,0:T(2,128)(2,1)}, u32[]{:S(2)}) copy-start(bf16[128,2,384]{2,1,0:T(2,128)(2,1)} %param.23) | copy-start | bytes 589828
  6.5 11.6 %copy-start.29 = (s32[128,1]{0,1:T(1,128)S(1)}, s32[128,1]{0,1:T(1,128)}, u32[]{:S(2)}) copy-start(s32[128,1]{0,1:T(1,128)} %param.18) | copy-start | bytes 1540
  6.5 37.2 %collective-permute-start = (bf16[128,2560]{1,0:T(8,128)(2,1)}, bf16[128,2560]{1,0:T(8,128)(2,1)}, u32[]{:S(2)}, u32[]{:S(2)}) collective-permute-start(bf16[128,2560]{1,0:T(8,128)(2,1)} %param.17), channel_id=1, source_target_pairs={{0,1},{1,2},{2,3},{3,4},{4,5},{5,6},{6,7},{7,0},{8,9},{9,10},{10,1... | collective-permute-start | bytes 1966088 | tf_op jit(solution)/shard_map/ppermute | solution.py:27
  9.2 34.5 %collective-permute-start.1 = (bf16[128,2560]{1,0:T(8,128)(2,1)}, bf16[128,2560]{1,0:T(8,128)(2,1)S(1)}, u32[]{:S(2)}, u32[]{:S(2)}) collective-permute-start(bf16[128,2560]{1,0:T(8,128)(2,1)} %param.17), channel_id=1, source_target_pairs={{0,7},{1,0},{2,1},{3,2},{4,3},{5,4},{6,5},{7,6},{8,15},{9,8},{10,9... | collective-permute-start | bytes 1966088 | tf_op jit(solution)/shard_map/ppermute | solution.py:32
  11.5 60.9 %all-to-all-start = ((bf16[8,2560,16]{1,2,0:T(8,128)(2,1)}), bf16[8,2560,16]{1,2,0:T(8,128)(2,1)S(1)}, u32[]{:S(2)}, u32[]{:S(2)}) async-start(bf16[8,2560,16]{1,2,0:T(8,128)(2,1)} %broadcast_in_dim.76), calls=%async_computation | async-start | bytes 1310720 | tf_op jit(solution)/shard_map/all_to_all | solution.py:47
  17.9 247.9 %all-gather.5.cloned.1.call-start = ((), (), s32[]{:S(2)}) async-start(), calls=%async_computation.2 | async-start | bytes 1769472 | tf_op jit(solution)/shard_map/all_gather | solution.py:73
  34.0 4.8 %copy-start.14 = (f32[4,384]{1,0:T(4,128)S(1)}, f32[4,384]{1,0:T(4,128)}, u32[]{:S(2)}) copy-start(f32[4,384]{1,0:T(4,128)} %param.24) | copy-start | bytes 18436
  34.0 4.8 %copy-start.30 = (f32[6]{0:T(128)S(1)}, f32[6]{0:T(128)}, u32[]{:S(2)}) copy-start(f32[6]{0:T(128)} %param.29) | copy-start | bytes 76
  34.0 4.9 %copy-start.31 = (u32[256]{0:T(256)S(1)}, u32[256]{0:T(256)}, u32[]{:S(2)}) copy-start(u32[256]{0:T(256)} %constant.144) | copy-start | bytes 3076
  34.0 6.1 %copy-start.21 = (f32[4,256]{1,0:T(4,128)S(1)}, f32[4,256]{1,0:T(4,128)}, u32[]{:S(2)}) copy-start(f32[4,256]{1,0:T(4,128)} %param.25) | copy-start | bytes 12292
  38.8 53.7 %copy-start.15 = (f32[6]{0:T(128)}, f32[6]{0:T(128)S(1)}, u32[]{:S(2)}) copy-start(f32[6]{0:T(128)S(1)} %neg.22) | copy-start | bytes 76
  40.2 2.7 copy-start.7
  43.8 7.9 %collective-permute-start.2 = (bf16[128,2560]{1,0:T(8,128)(2,1)}, bf16[128,2560]{1,0:T(8,128)(2,1)S(1)}, u32[]{:S(2)}, u32[]{:S(2)}) collective-permute-start(bf16[128,2560]{1,0:T(8,128)(2,1)} %collective-permute-done), channel_id=1, source_target_pairs={{0,1},{1,2},{2,3},{3,4},{4,5},{5,6},{6,7},{7,0},{8,9},{9,10},{10,1... | collective-permute-start | bytes 1966088 | tf_op jit(solution)/shard_map/ppermute | solution.py:27
  43.8 10.3 %collective-permute-start.3 = (bf16[128,2560]{1,0:T(8,128)(2,1)S(1)}, bf16[128,2560]{1,0:T(8,128)(2,1)S(1)}, u32[]{:S(2)}, u32[]{:S(2)}) collective-permute-start(bf16[128,2560]{1,0:T(8,128)(2,1)S(1)} %collective-permute-done.1), channel_id=1, source_target_pairs={{0,7},{1,0},{2,1},{3,2},{4,3},{5,4},{6,5},{7,6},{8,15},{9,8},{10,9... | collective-permute-start | bytes 1966088 | tf_op jit(solution)/shard_map/ppermute | solution.py:32
  51.6 9.9 %collective-permute-start.4 = (bf16[128,2560]{1,0:T(8,128)(2,1)S(1)}, bf16[128,2560]{1,0:T(8,128)(2,1)S(1)}, u32[]{:S(2)}, u32[]{:S(2)}) collective-permute-start(bf16[128,2560]{1,0:T(8,128)(2,1)S(1)} %collective-permute-done.2), channel_id=1, source_target_pairs={{0,1},{1,2},{2,3},{3,4},{4,5},{5,6},{6,7},{7,0},{8,9},{9,10},{10,1... | collective-permute-start | bytes 1966088 | tf_op jit(solution)/shard_map/ppermute | solution.py:27
  54.1 10.8 %collective-permute-start.5 = (bf16[128,2560]{1,0:T(8,128)(2,1)S(1)}, bf16[128,2560]{1,0:T(8,128)(2,1)S(1)}, u32[]{:S(2)}, u32[]{:S(2)}) collective-permute-start(bf16[128,2560]{1,0:T(8,128)(2,1)S(1)} %collective-permute-done.3), channel_id=1, source_target_pairs={{0,7},{1,0},{2,1},{3,2},{4,3},{5,4},{6,5},{7,6},{8,15},{9,8},{10,9... | collective-permute-start | bytes 1966088 | tf_op jit(solution)/shard_map/ppermute | solution.py:32
  61.5 10.0 %collective-permute-start.6 = (bf16[128,2560]{1,0:T(8,128)(2,1)S(1)}, bf16[128,2560]{1,0:T(8,128)(2,1)S(1)}, u32[]{:S(2)}, u32[]{:S(2)}) collective-permute-start(bf16[128,2560]{1,0:T(8,128)(2,1)S(1)} %collective-permute-done.4), channel_id=1, source_target_pairs={{0,1},{1,2},{2,3},{3,4},{4,5},{5,6},{6,7},{7,0},{8,9},{9,10},{10,1... | collective-permute-start | bytes 1966088 | tf_op jit(solution)/shard_map/ppermute | solution.py:27
  72.4 5.1 %copy-start.6 = (bf16[320,8,2,384]{3,1,2,0:T(8,128)(2,1)S(1)}, bf16[320,8,2,384]{3,1,2,0:T(8,128)(2,1)}, u32[]{:S(2)}) copy-start(bf16[320,8,2,384]{3,1,2,0:T(8,128)(2,1)} %copy.123) | copy-start | bytes 11796484
  83.7 5.6 %copy-start.4 = (f32[1024,768]{1,0:T(8,128)}, f32[1024,768]{1,0:T(8,128)S(1)}, u32[]{:S(2)}) copy-start(f32[1024,768]{1,0:T(8,128)S(1)} %convolution_add_fusion) | copy-start | bytes 9437188
  83.7 8.8 %copy-start.13 = (bf16[2560,6]{0,1:T(8,128)(2,1)S(1)}, bf16[2560,6]{0,1:T(8,128)(2,1)}, u32[]{:S(2)}) copy-start(bf16[2560,6]{0,1:T(8,128)(2,1)} %param.21) | copy-start | bytes 92164
  83.7 8.8 %copy-start.23 = (f32[6]{0:T(128)S(1)}, f32[6]{0:T(128)}, u32[]{:S(2)}) copy-start(f32[6]{0:T(128)} %param.28) | copy-start | bytes 76
  83.8 26.6 %collective-permute-start.7 = (f32[3,384]{1,0:T(4,128)S(1)}, f32[3,384]{1,0:T(4,128)S(1)}, u32[]{:S(2)}, u32[]{:S(2)}) collective-permute-start(f32[3,384]{1,0:T(4,128)S(1)} %slice.215), channel_id=1, source_target_pairs={{0,8},{8,16},{16,24},{24,32},{32,40},{40,48},{48,56},{56,64},{64,7... | collective-permute-start | bytes 13832 | tf_op jit(solution)/shard_map/ppermute | solution.py:59
  89.3 17.6 %collective-permute-start.8 = (f32[3,256]{1,0:T(4,128)S(1)}, f32[3,256]{1,0:T(4,128)S(1)}, u32[]{:S(2)}, u32[]{:S(2)}) collective-permute-start(f32[3,256]{1,0:T(4,128)S(1)} %slice.221), channel_id=1, source_target_pairs={{0,8},{8,16},{16,24},{24,32},{32,40},{40,48},{48,56},{56,64},{64,7... | collective-permute-start | bytes 9224 | tf_op jit(solution)/shard_map/ppermute | solution.py:59
  106.9 0.7 copy-start.27
  108.3 1.0 copy-start.2
  109.3 1.8 slice-start
  109.3 1.8 copy-start.22
  122.3 0.6 copy-start.12
  123.0 4.9 %copy-start.8 = (f32[256,6]{0,1:T(8,128)S(1)}, f32[256,6]{0,1:T(8,128)}, u32[]{:S(2)}) copy-start(f32[256,6]{0,1:T(8,128)} %get-tuple-element.235) | copy-start | bytes 18436 | tf_op jit(solution)/shard_map/while
  123.0 4.9 %copy-start.9 = (f32[256,6]{0,1:T(8,128)S(1)}, f32[256,6]{0,1:T(8,128)}, u32[]{:S(2)}) copy-start(f32[256,6]{0,1:T(8,128)} %get-tuple-element.236) | copy-start | bytes 18436 | tf_op jit(solution)/shard_map/while
  145.1 0.6 copy-start.12
  145.7 4.9 %copy-start.8 = (f32[256,6]{0,1:T(8,128)S(1)}, f32[256,6]{0,1:T(8,128)}, u32[]{:S(2)}) copy-start(f32[256,6]{0,1:T(8,128)} %get-tuple-element.235) | copy-start | bytes 18436 | tf_op jit(solution)/shard_map/while
  145.7 4.9 %copy-start.9 = (f32[256,6]{0,1:T(8,128)S(1)}, f32[256,6]{0,1:T(8,128)}, u32[]{:S(2)}) copy-start(f32[256,6]{0,1:T(8,128)} %get-tuple-element.236) | copy-start | bytes 18436 | tf_op jit(solution)/shard_map/while
  167.9 0.6 copy-start.12
  168.5 4.9 %copy-start.8 = (f32[256,6]{0,1:T(8,128)S(1)}, f32[256,6]{0,1:T(8,128)}, u32[]{:S(2)}) copy-start(f32[256,6]{0,1:T(8,128)} %get-tuple-element.235) | copy-start | bytes 18436 | tf_op jit(solution)/shard_map/while
  168.5 4.9 %copy-start.9 = (f32[256,6]{0,1:T(8,128)S(1)}, f32[256,6]{0,1:T(8,128)}, u32[]{:S(2)}) copy-start(f32[256,6]{0,1:T(8,128)} %get-tuple-element.236) | copy-start | bytes 18436 | tf_op jit(solution)/shard_map/while
  190.7 0.6 copy-start.12
  191.3 4.9 %copy-start.8 = (f32[256,6]{0,1:T(8,128)S(1)}, f32[256,6]{0,1:T(8,128)}, u32[]{:S(2)}) copy-start(f32[256,6]{0,1:T(8,128)} %get-tuple-element.235) | copy-start | bytes 18436 | tf_op jit(solution)/shard_map/while
  191.3 4.9 %copy-start.9 = (f32[256,6]{0,1:T(8,128)S(1)}, f32[256,6]{0,1:T(8,128)}, u32[]{:S(2)}) copy-start(f32[256,6]{0,1:T(8,128)} %get-tuple-element.236) | copy-start | bytes 18436 | tf_op jit(solution)/shard_map/while
  208.1 13.0 %copy-start.11 = (f32[1024,6]{0,1:T(8,128)S(1)}, f32[1024,6]{0,1:T(8,128)}, u32[]{:S(2)}) copy-start(f32[1024,6]{0,1:T(8,128)} %get-tuple-element.181) | copy-start | bytes 73732
  208.1 13.0 %copy-start.16 = (f32[6]{0:T(128)S(1)}, f32[6]{0:T(128)}, u32[]{:S(2)}) copy-start(f32[6]{0:T(128)} %copy-done.15) | copy-start | bytes 76
  208.1 15.2 %copy-start.24 = (f32[1,1,6]{2,1,0:T(1,128)S(1)}, f32[1,1,6]{2,1,0:T(1,128)}, u32[]{:S(2)}) copy-start(f32[1,1,6]{2,1,0:T(1,128)} %get-tuple-element.177) | copy-start | bytes 76
  218.6 0.9 copy-start.1
  237.3 28.6 %copy-start.17 = (f32[6]{0:T(128)S(1)}, f32[6]{0:T(128)}, u32[]{:S(2)}) copy-start(f32[6]{0:T(128)} %get-tuple-element.176) | copy-start | bytes 76
  237.3 28.6 %copy-start.18 = (f32[6]{0:T(128)S(1)}, f32[6]{0:T(128)}, u32[]{:S(2)}) copy-start(f32[6]{0:T(128)} %get-tuple-element.178) | copy-start | bytes 76
  237.3 28.6 %copy-start.19 = (f32[6]{0:T(128)S(1)}, f32[6]{0:T(128)}, u32[]{:S(2)}) copy-start(f32[6]{0:T(128)} %get-tuple-element.179) | copy-start | bytes 76
  237.3 28.5 %copy-start.20 = (f32[6]{0:T(128)S(1)}, f32[6]{0:T(128)}, u32[]{:S(2)}) copy-start(f32[6]{0:T(128)} %get-tuple-element.180) | copy-start | bytes 76
  237.3 28.5 %copy-start.26 = (f32[6]{0:T(128)S(1)}, f32[6]{0:T(128)}, u32[]{:S(2)}) copy-start(f32[6]{0:T(128)} %get-tuple-element.175) | copy-start | bytes 76
  265.8 2.2 copy-start.3
  268.0 1.4 copy-start.5
  268.0 1.4 copy-start.28
  273.1 16.4 %copy-start.25 = (f32[384]{0:T(512)S(1)}, f32[384]{0:T(512)}, u32[]{:S(2)}) copy-start(f32[384]{0:T(512)} %param.31) | copy-start | bytes 4612
Sparse Core Ops, SparseCore 0:
  221.1 44.6 all-gather.4
